TPU v7x, 32 devices: a whole 2x2x4 slice. The times are simulated.
32 devices in a mesh: dp: 4 (over y, core), wide: 8 (over z, x).
Axes of the slice: x: 2, y: 2, z: 4, core: 2. Of those that a mesh axis runs over, the one named last changes fastest.
Arguments:
- fields: bfloat16 [16, 64, 128, 1280], P('dp', 'wide'), may hold values from -6 to 6
- targets: bfloat16 [16, 64, 128, 1280], P('dp', 'wide'), may hold values from -6 to 6
- patch_mask: int32 [16, 64, 128], P('dp', 'wide'), may hold values from 0 to 1, as said below
- channel_mask: int32 [16, 20], P('dp'), may hold values from 0 to 1, as said below
- embed_weight: float32 [1280, 768], P(('dp', 'wide')), may hold values from -0.15625 to 0.15625
- head_weight: float32 [768, 1280], P(('dp', 'wide')), may hold values from -0.21875 to 0.21875
- expand_weight: float32 [768, 3072], P(('dp', 'wide')), may hold values from -0.21875 to 0.21875
- project_weight: float32 [3072, 768], P(('dp', 'wide')), may hold values from -0.109375 to 0.109375
- spectral_weight: float32 [2, 2, 768, 96], P(None, None, ('dp', 'wide')), may hold values from -0.4375 to 0.4375
- small_params: float32 [14, 768], P(None, ('dp', 'wide')), may hold values from -1.2 to 1.3
- embed_moment: float32 [1280, 768], P(('dp', 'wide'))
- head_moment: float32 [768, 1280], P(('dp', 'wide'))
- expand_moment: float32 [768, 3072], P(('dp', 'wide'))
- project_moment: float32 [3072, 768], P(('dp', 'wide'))
- spectral_moment: float32 [2, 2, 768, 96], P(None, None, ('dp', 'wide'))
- small_moment: float32 [14, 768], P(None, ('dp', 'wide'))
- embed_square: float32 [1280, 768], P(('dp', 'wide'))
- head_square: float32 [768, 1280], P(('dp', 'wide'))
- expand_square: float32 [768, 3072], P(('dp', 'wide'))
- project_square: float32 [3072, 768], P(('dp', 'wide'))
- spectral_square: float32 [2, 2, 768, 96], P(None, None, ('dp', 'wide'))
- small_square: float32 [14, 768], P(None, ('dp', 'wide'))
Outputs:
- loss: float32 [], replicated
- grad_norm: float32 [], replicated
- embed_next: float32 [1280, 768], P(('dp', 'wide'))
- embed_moment_next: float32 [1280, 768], P(('dp', 'wide'))
- embed_square_next: float32 [1280, 768], P(('dp', 'wide'))
- head_next: float32 [768, 1280], P(('dp', 'wide'))
- head_moment_next: float32 [768, 1280], P(('dp', 'wide'))
- head_square_next: float32 [768, 1280], P(('dp', 'wide'))
- expand_next: float32 [768, 3072], P(('dp', 'wide'))
- expand_moment_next: float32 [768, 3072], P(('dp', 'wide'))
- expand_square_next: float32 [768, 3072], P(('dp', 'wide'))
- project_next: float32 [3072, 768], P(('dp', 'wide'))
- project_moment_next: float32 [3072, 768], P(('dp', 'wide'))
- project_square_next: float32 [3072, 768], P(('dp', 'wide'))
- spectral_next: float32 [2, 2, 768, 96], P(None, None, ('dp', 'wide'))
- spectral_moment_next: float32 [2, 2, 768, 96], P(None, None, ('dp', 'wide'))
- spectral_square_next: float32 [2, 2, 768, 96], P(None, None, ('dp', 'wide'))
- small_next: float32 [14, 768], P(None, ('dp', 'wide'))
- small_moment_next: float32 [14, 768], P(None, ('dp', 'wide'))
- small_square_next: float32 [14, 768], P(None, ('dp', 'wide'))
Inputs may be any that keep to these rules, and one draw needn't show every extreme that they name: `patch_mask`: A sample of the coarse group other than the first has valid patches only in its first 32 rows and 64 columns; the first grid row of the first sample is all valid. `channel_mask`: the first sample observes every channel.
All inputs are finite; a program needn't handle non-finite values.
Results may differ from a plain program's by a relative error of at most 0.0055.
The roundings to bfloat16 on the way count: a program that leaves them out, or rounds other values in their place, can miss the bound.
Values may be sent and summed in bfloat16 or wider, within the bound.
A program may use at most 512 MiB of HBM per device.

v0:
```python
import jax
import jax.numpy as jnp
from jax import lax
from jax.sharding import PartitionSpec as P

EPSILON = 1e-06
SHRINK = 0.01
BETA_ONE = 0.9
BETA_TWO = 0.95
RATES = (0.08, 0.1, 0.1, 0.05, 0.3, 0.5)
DECAYS = (0.1, 0.1, 0.1, 0.1, 0.1, 0.0)


def layer_norm(values, gain, shift):
    centred = values - jnp.mean(values, axis=-1, keepdims=True)
    spread = jnp.mean(centred * centred, axis=-1, keepdims=True)
    return centred * lax.rsqrt(spread + EPSILON) * gain + shift


def make_tables(grid_height, grid_width):
    across = jnp.arange(grid_width, dtype=jnp.int32)
    freqs = jnp.arange(grid_width // 2, dtype=jnp.int32)
    angles = (
        2.0
        * jnp.pi
        / grid_width
        * (across[:, None] * freqs[None, :] % grid_width).astype(jnp.float32)
    )
    row_table = (
        jnp.stack([jnp.cos(angles), -jnp.sin(angles)], axis=1) / jnp.sqrt(jnp.float32(grid_width))
    ).astype(jnp.bfloat16)
    doubling = jnp.where(freqs == 0, 1.0, 2.0).astype(jnp.float32)
    inv_table = (row_table.astype(jnp.float32) * doubling).astype(jnp.bfloat16)
    down = jnp.arange(grid_height, dtype=jnp.int32)
    col_angles = (
        2.0
        * jnp.pi
        / grid_height
        * (down[:, None] * down[None, :] % grid_height).astype(jnp.float32)
    )
    cosine = jnp.cos(col_angles) / jnp.sqrt(jnp.float32(grid_height))
    sine = jnp.sin(col_angles) / jnp.sqrt(jnp.float32(grid_height))
    col_table = jnp.stack([jnp.stack([cosine, sine]), jnp.stack([-sine, cosine])]).astype(
        jnp.bfloat16
    )
    return (row_table, inv_table, col_table)


def complex_mix(spec, weight, bias):
    shape = spec.shape
    block_size = weight.shape[2]
    nblocks = weight.shape[1] // block_size
    blocks = spec.reshape(-1, 2, shape[-2], nblocks, block_size)
    kernel = weight.reshape(2, nblocks, block_size, block_size)
    prods = jnp.einsum("xakbi,cbij->xackbj", blocks, kernel, preferred_element_type=jnp.float32)
    real_part = prods[:, 0, 0] - prods[:, 1, 1]
    imag_part = prods[:, 0, 1] + prods[:, 1, 0]
    return jnp.stack([real_part, imag_part], axis=1).reshape(shape) + bias[:, None, :]


def complex_back(grad_out, spec, weight):
    shape = spec.shape
    block_size = weight.shape[2]
    nblocks = weight.shape[1] // block_size
    blocks = spec.reshape(-1, 2, shape[-2], nblocks, block_size)
    grads_blocks = grad_out.reshape(-1, 2, shape[-2], nblocks, block_size)
    kernel = weight.reshape(2, nblocks, block_size, block_size)
    prods = jnp.einsum(
        "xokbj,cbij->xockbi", grads_blocks, kernel, preferred_element_type=jnp.float32
    )
    real_part = prods[:, 0, 0] + prods[:, 1, 1]
    imag_part = prods[:, 1, 0] - prods[:, 0, 1]
    grad_spec = jnp.stack([real_part, imag_part], axis=1).reshape(shape)
    cross = jnp.einsum(
        "xakbi,xokbj->aobij", blocks, grads_blocks, preferred_element_type=jnp.float32
    )
    grad_weight = jnp.stack([cross[0, 0] + cross[1, 1], cross[0, 1] - cross[1, 0]]).reshape(
        weight.shape
    )
    grad_bias = jnp.sum(
        grad_out.reshape(-1, 2, shape[-2], shape[-1]), axis=(0, 2), dtype=jnp.float32
    )
    return (grad_spec, grad_weight, grad_bias)


def forward_layer(inputs, used, tables, layout):
    embed_used, head_used, expand_used, project_used, spectral_used, small_used = used
    row_table, inv_table, col_table = tables
    samples, rows_dev, grid_width = layout
    tokens = inputs.shape[0]
    width_model = embed_used.shape[1]
    hidden_zero = jnp.dot(inputs, embed_used, preferred_element_type=jnp.float32) + small_used[4]
    normed_one = layer_norm(hidden_zero, small_used[0], small_used[1])
    normed_low = normed_one.astype(jnp.bfloat16).reshape(samples, rows_dev, grid_width, width_model)
    rows_freq = jnp.einsum(
        "srwd,wak->srakd", normed_low, row_table, preferred_element_type=jnp.float32
    ).astype(jnp.bfloat16)
    rows_moved = lax.all_to_all(rows_freq, "wide", split_axis=3, concat_axis=1, tiled=True)
    spectrum = jnp.einsum(
        "oaxi,siakd->sxokd", col_table, rows_moved, preferred_element_type=jnp.float32
    ).astype(jnp.bfloat16)
    first_pre = complex_mix(spectrum, spectral_used[0], small_used[10:12])
    first_act = jax.nn.relu(first_pre).astype(jnp.bfloat16)
    second_pre = complex_mix(first_act, spectral_used[1], small_used[12:14])
    shrunk = (second_pre - jnp.clip(second_pre, -SHRINK, SHRINK)).astype(jnp.bfloat16)
    back_cols = jnp.einsum(
        "aoxi,sxakd->siokd", col_table, shrunk, preferred_element_type=jnp.float32
    ).astype(jnp.bfloat16)
    cols_moved = lax.all_to_all(back_cols, "wide", split_axis=1, concat_axis=3, tiled=True)
    filtered = jnp.einsum(
        "wak,srakd->srwd", inv_table, cols_moved, preferred_element_type=jnp.float32
    ).reshape(tokens, width_model)
    hidden_one = hidden_zero + filtered + normed_one
    normed_two = layer_norm(hidden_one, small_used[2], small_used[3]).astype(jnp.bfloat16)
    expand_pre = jnp.dot(normed_two, expand_used, preferred_element_type=jnp.float32) + small_used[
        6:10
    ].reshape(-1)
    expand_act = jax.nn.gelu(expand_pre, approximate=False).astype(jnp.bfloat16)
    hidden_two = (
        hidden_one
        + jnp.dot(expand_act, project_used, preferred_element_type=jnp.float32)
        + small_used[5]
    )
    hidden_low = hidden_two.astype(jnp.bfloat16)
    predict = jnp.dot(hidden_low, head_used, preferred_element_type=jnp.float32)
    kept = (
        hidden_zero,
        spectrum,
        first_pre,
        first_act,
        second_pre,
        hidden_one,
        normed_two,
        expand_pre,
        expand_act,
        hidden_low,
    )
    return (predict, kept)


def backward_layer(grad_predict, inputs, used, tables, layout, kept):
    embed_used, head_used, expand_used, project_used, spectral_used, small_used = used
    row_table, inv_table, col_table = tables
    samples, rows_dev, grid_width = layout
    (
        hidden_zero,
        spectrum,
        first_pre,
        first_act,
        second_pre,
        hidden_one,
        normed_two,
        expand_pre,
        expand_act,
        hidden_low,
    ) = kept
    tokens = inputs.shape[0]
    width_model = embed_used.shape[1]
    grad_low = grad_predict.astype(jnp.bfloat16)
    grad_head = jnp.einsum("td,tp->dp", hidden_low, grad_low, preferred_element_type=jnp.float32)
    grad_two = jnp.einsum("tp,dp->td", grad_low, head_used, preferred_element_type=jnp.float32)
    grad_branch = grad_two.astype(jnp.bfloat16)
    grad_project = jnp.einsum(
        "tf,td->fd", expand_act, grad_branch, preferred_element_type=jnp.float32
    )
    bias_project = jnp.sum(grad_branch, axis=0, dtype=jnp.float32)
    grad_act = jnp.einsum(
        "td,fd->tf", grad_branch, project_used, preferred_element_type=jnp.float32
    )
    gelu_pull = jax.vjp(lambda values: jax.nn.gelu(values, approximate=False), expand_pre)[1]
    grad_pre = gelu_pull(grad_act)[0].astype(jnp.bfloat16)
    grad_expand = jnp.einsum("td,tf->df", normed_two, grad_pre, preferred_element_type=jnp.float32)
    bias_expand = jnp.sum(grad_pre, axis=0, dtype=jnp.float32)
    grad_normed = jnp.einsum("tf,df->td", grad_pre, expand_used, preferred_element_type=jnp.float32)
    second_pull = jax.vjp(layer_norm, hidden_one, small_used[2], small_used[3])[1]
    back_one, gain_two, shift_two = second_pull(grad_normed)
    grad_one = grad_two + back_one
    grad_filter = grad_one.astype(jnp.bfloat16).reshape(samples, rows_dev, grid_width, width_model)
    grad_cols = jnp.einsum(
        "wak,srwd->srakd", inv_table, grad_filter, preferred_element_type=jnp.float32
    ).astype(jnp.bfloat16)
    grad_moved = lax.all_to_all(grad_cols, "wide", split_axis=3, concat_axis=1, tiled=True)
    grad_shrunk = jnp.einsum(
        "aoxi,siokd->sxakd", col_table, grad_moved, preferred_element_type=jnp.float32
    )
    grad_second = jnp.where(jnp.abs(second_pre) > SHRINK, grad_shrunk, 0.0).astype(jnp.bfloat16)
    grad_first_act, weight_two, bias_two = complex_back(grad_second, first_act, spectral_used[1])
    grad_first = jnp.where(first_pre > 0.0, grad_first_act, 0.0).astype(jnp.bfloat16)
    grad_spectrum, weight_one, bias_one = complex_back(grad_first, spectrum, spectral_used[0])
    grad_rows = jnp.einsum(
        "oaxi,sxokd->siakd",
        col_table,
        grad_spectrum.astype(jnp.bfloat16),
        preferred_element_type=jnp.float32,
    ).astype(jnp.bfloat16)
    grad_back = lax.all_to_all(grad_rows, "wide", split_axis=1, concat_axis=3, tiled=True)
    grad_normed_one = (
        jnp.einsum(
            "wak,srakd->srwd", row_table, grad_back, preferred_element_type=jnp.float32
        ).reshape(tokens, width_model)
        + grad_one
    )
    first_pull = jax.vjp(layer_norm, hidden_zero, small_used[0], small_used[1])[1]
    back_zero, gain_one, shift_one = first_pull(grad_normed_one)
    grad_zero = (grad_one + back_zero).astype(jnp.bfloat16)
    grad_embed = jnp.einsum("tp,td->pd", inputs, grad_zero, preferred_element_type=jnp.float32)
    bias_embed = jnp.sum(grad_zero, axis=0, dtype=jnp.float32)
    grad_spectral = jnp.stack([weight_one, weight_two])
    grad_small = jnp.concatenate(
        [
            jnp.stack([gain_one, shift_one, gain_two, shift_two, bias_embed, bias_project]),
            bias_expand.reshape(4, width_model),
            bias_one,
            bias_two,
        ],
        axis=0,
    )
    return (
        lax.psum_scatter(grad_embed, ("dp", "wide"), scatter_dimension=0, tiled=True),
        lax.psum_scatter(grad_head, ("dp", "wide"), scatter_dimension=0, tiled=True),
        lax.psum_scatter(grad_expand, ("dp", "wide"), scatter_dimension=0, tiled=True),
        lax.psum_scatter(grad_project, ("dp", "wide"), scatter_dimension=0, tiled=True),
        lax.psum_scatter(grad_spectral, ("dp", "wide"), scatter_dimension=2, tiled=True),
        lax.psum_scatter(grad_small, ("dp", "wide"), scatter_dimension=1, tiled=True),
    )


def adam_update(master, moment, square, grad, factor, rate, decay):
    clipped = grad * factor
    moment_next = BETA_ONE * moment + (1.0 - BETA_ONE) * clipped
    square_next = BETA_TWO * square + (1.0 - BETA_TWO) * clipped * clipped
    ratio = (
        moment_next / (1.0 - BETA_ONE**10) / (jnp.sqrt(square_next / (1.0 - BETA_TWO**10)) + 1e-08)
    )
    return (master - rate * (ratio + decay * master), moment_next, square_next)


def shards(
    fields,
    targets,
    patch_mask,
    channel_mask,
    embed_weight,
    head_weight,
    expand_weight,
    project_weight,
    spectral_weight,
    small_params,
    embed_moment,
    head_moment,
    expand_moment,
    project_moment,
    spectral_moment,
    small_moment,
    embed_square,
    head_square,
    expand_square,
    project_square,
    spectral_square,
    small_square,
):
    masters = (
        embed_weight,
        head_weight,
        expand_weight,
        project_weight,
        spectral_weight,
        small_params,
    )
    moments = (
        embed_moment,
        head_moment,
        expand_moment,
        project_moment,
        spectral_moment,
        small_moment,
    )
    squares = (
        embed_square,
        head_square,
        expand_square,
        project_square,
        spectral_square,
        small_square,
    )
    gathered = (
        lax.all_gather(embed_weight.astype(jnp.bfloat16), ("dp", "wide"), axis=0, tiled=True),
        lax.all_gather(head_weight.astype(jnp.bfloat16), ("dp", "wide"), axis=0, tiled=True),
        lax.all_gather(expand_weight.astype(jnp.bfloat16), ("dp", "wide"), axis=0, tiled=True),
        lax.all_gather(project_weight.astype(jnp.bfloat16), ("dp", "wide"), axis=0, tiled=True),
        lax.all_gather(spectral_weight.astype(jnp.bfloat16), ("dp", "wide"), axis=2, tiled=True),
        lax.all_gather(small_params.astype(jnp.bfloat16), ("dp", "wide"), axis=1, tiled=True),
    )
    used = tuple(gathered[:5]) + (gathered[5].astype(jnp.float32),)
    samples, rows_dev, grid_width, patch_dim = fields.shape
    grid_height = rows_dev * lax.axis_size("wide")
    tables = make_tables(grid_height, grid_width)
    layout = (samples, rows_dev, grid_width)
    channels = channel_mask.shape[1]
    pixels = patch_dim // channels
    tokens = samples * rows_dev * grid_width
    valid_patch = patch_mask.astype(jnp.float32)
    channel_on = channel_mask.astype(jnp.float32)
    local_counts = jnp.sum(channel_on * jnp.sum(valid_patch, axis=(1, 2))[:, None], axis=0) * pixels
    counts = lax.psum(local_counts, ("dp", "wide"))
    scale_cols = jnp.repeat(1.0 / (channels * counts), pixels)
    inputs = (fields * patch_mask[..., None].astype(jnp.bfloat16)).reshape(tokens, patch_dim)
    predict, kept = forward_layer(inputs, used, tables, layout)
    weighted = (
        valid_patch[..., None] * jnp.repeat(channel_on, pixels, axis=1)[:, None, None, :]
    ).reshape(tokens, patch_dim)
    errors = predict - targets.reshape(tokens, patch_dim).astype(jnp.float32)
    grad_predict = 2.0 * errors * weighted * scale_cols
    reduced = backward_layer(grad_predict, inputs, used, tables, layout, kept)
    local_square = sum((jnp.sum(grad * grad) for grad in reduced))
    local_error = jnp.sum(
        (errors * errors * weighted).reshape(tokens, channels, pixels), axis=(0, 2)
    )
    total_square, error_sums = lax.psum((local_square, local_error), ("dp", "wide"))
    grad_norm = jnp.sqrt(total_square)
    loss = jnp.sum(error_sums / counts) / channels
    batch = samples * lax.axis_size("dp")
    clip_level = 0.25 / jnp.sqrt(jnp.float32(batch * grid_height * grid_width))
    factor = jnp.minimum(1.0, clip_level / grad_norm)
    results = [loss, grad_norm]
    for index in range(6):
        results.extend(
            adam_update(
                masters[index],
                moments[index],
                squares[index],
                reduced[index],
                factor,
                RATES[index],
                DECAYS[index],
            )
        )
    return tuple(results)


def solution(mesh):
    placed = (
        P("dp", "wide", None, None),
        P("dp", "wide", None, None),
        P("dp", "wide", None),
        P("dp", None),
        P(("dp", "wide"), None),
        P(("dp", "wide"), None),
        P(("dp", "wide"), None),
        P(("dp", "wide"), None),
        P(None, None, ("dp", "wide"), None),
        P(None, ("dp", "wide")),
        P(("dp", "wide"), None),
        P(("dp", "wide"), None),
        P(("dp", "wide"), None),
        P(("dp", "wide"), None),
        P(None, None, ("dp", "wide"), None),
        P(None, ("dp", "wide")),
        P(("dp", "wide"), None),
        P(("dp", "wide"), None),
        P(("dp", "wide"), None),
        P(("dp", "wide"), None),
        P(None, None, ("dp", "wide"), None),
        P(None, ("dp", "wide")),
    )
    return jax.shard_map(
        shards,
        mesh=mesh,
        in_specs=placed,
        out_specs=(
            P(),
            P(),
            P(("dp", "wide"), None),
            P(("dp", "wide"), None),
            P(("dp", "wide"), None),
            P(("dp", "wide"), None),
            P(("dp", "wide"), None),
            P(("dp", "wide"), None),
            P(("dp", "wide"), None),
            P(("dp", "wide"), None),
            P(("dp", "wide"), None),
            P(("dp", "wide"), None),
            P(("dp", "wide"), None),
            P(("dp", "wide"), None),
            P(None, None, ("dp", "wide"), None),
            P(None, None, ("dp", "wide"), None),
            P(None, None, ("dp", "wide"), None),
            P(None, ("dp", "wide")),
            P(None, ("dp", "wide")),
            P(None, ("dp", "wide")),
        ),
        check_vma=False,
    )
```

profile of v0, /device:TPU:0, one launch (start us, length us, event | category | flops | bytes accessed | tf_op | source)
XLA Modules:
  0.0 1966.7 jit_solution(1096114445009783065)
XLA Ops:
  9.5 70.5 %all-gather = bf16[32,24,14]{1,2,0:T(8,128)(2,1)S(1)} all-gather(bf16[1,24,14]{1,2,0:T(8,128)(2,1)S(1)} %convert_bitcast_fusion.3), channel_id=1, replica_groups=mesh['dp'=4,'wide'=8] {'dp','wide'}, dimensions={0}, use_global_device_ids=true | all-gather | bytes 22176 | tf_op jit(solution)/shard_map/all_gather | solution.py:292
  82.7 11.1 broadcast_multiply_fusion
  93.8 11.8 add_reduce_fusion
  112.4 6.2 copy.216
  124.3 215.2 %all_gather.20 = bf16[2,2,768,96]{3,2,1,0:T(8,128)(2,1)S(1)} all-gather(bf16[2,2,24,96]{3,2,1,0:T(8,128)(2,1)S(1)} %convert_element_type.190), channel_id=1, replica_groups=mesh['dp'=4,'wide'=8] {'dp','wide'}, dimensions={2}, use_global_device_ids=true | all-gather | bytes 608256 | tf_op jit(solution)/shard_map/all_gather | solution.py:291
  339.9 7.1 fusion.25
  346.9 6.3 copy.218
  353.2 15.2 reshape.647
  368.5 22.8 %convolution_bitcast_fusion.3 = f32[256,2,2,8,8,96]{0,5,2,3,1,4:T(8,128)} fusion(bf16[256,2,8,8,96,1]{4,3,2,1,0,5:T(8,128)(2,1)} %bitcast.304, bf16[2,8,96,96,1,1]{3,2,1,0,5,4:T(8,128)(2,1)S(1)} %bitcast.320), kind=kOutput, calls=%fused_computation.68 | convolution fusion | flops 1207959552 | bytes 31752192 | tf_op jit(solution)/shard_map/xakbi,cbij->xackbj/dot_general | solution.py:55
  391.2 5.7 fusion.156
  397.0 11.4 fusion.155
  408.4 12.1 convolution_bitcast_fusion.2
  420.4 14.8 slice_subtract_fusion.2
  435.3 8.3 copy.227
  443.6 9.6 sub.155
  453.2 7.4 copy.229
  460.6 8.3 copy.228
  468.9 9.6 add.401
  486.0 15.7 copy.232
  501.7 4.9 all-to-all-start.1
  508.3 174.4 %psum.22 = f32[20]{0:T(128)S(1)} all-reduce(f32[20]{0:T(128)S(1)} %broadcast_multiply_fusion.3), channel_id=1, replica_groups=mesh['dp'=4,'wide'=8] {'dp','wide'}, use_global_device_ids=true, to_apply=%region_9.10 | all-reduce | flops 20 | bytes 160 | tf_op jit(solution)/shard_map/psum | solution.py:305
  690.1 8.2 fusion.127
  704.3 135.3 %multiply_convert_fusion = (bf16[4096,3072]{1,0:T(8,128)(2,1)}, f32[4096,3072]{1,0:T(8,128)}, f32[4096,3072]{1,0:T(8,128)}) fusion(f32[3072]{0:T(1024)S(1)} %add.410, bf16[768,3072]{1,0:T(8,128)(2,1)} %all-gather.8.cloned.1.call-done, f32[4096,768]{1,0:T(8,128)} %copy-done.1, f32[768]{0:T(1024)S(1)} %copy-done.81, f32[768]{0:T(1024)S(1)} %copy-done.63, ...), kind=kOutput, calls=%fused_computation.4 | convolution fusion | flops 20173553664 | bytes 143181824 | tf_op jit(solution)/shard_map/dot_general | solution.py:115
  839.7 27.6 %add_convert_fusion.2 = bf16[4096,768]{1,0:T(8,128)(2,1)} fusion(f32[4096,768]{1,0:T(8,128)} %copy-done.1, bf16[4096,3072]{1,0:T(8,128)(2,1)} %get-tuple-element.123, bf16[3072,768]{1,0:T(8,128)(2,1)} %all-gather.10.cloned.1.call-done, f32[768]{0:T(1024)S(1)} %copy-done.83), kind=kOutput, calls=%fused_computation.56 | convolution fusion | flops 19336790016 | bytes 48761856 | tf_op jit(solution)/shard_map/dot_general | solution.py:121
  867.4 16.8 fusion.10
  884.2 11.1 fusion.131
  895.3 54.2 %convert_reduce_fusion = (f32[3072]{0:T(1024)}, bf16[4096,3072]{1,0:T(8,128)(2,1)}) fusion(f32[4096,3072]{1,0:T(8,128)} %get-tuple-element.124, bf16[3072,768]{1,0:T(8,128)(2,1)} %all-gather.10.cloned.1.call-done, f32[4096,768]{1,0:T(8,128)} %fusion.131, f32[4096,3072]{1,0:T(8,128)} %get-tuple-element.150, f32[3072]{0:T(1024)S(1)} %add.410), kind=kOutput, calls=%fused_computation.2 | convolution fusion | flops 19544403968 | bytes 143155200 | tf_op jit(solution)/shard_map/td,fd->tf/dot_general | solution.py:167
  949.5 27.8 %multiply_reduce_fusion = (f32[768]{0:T(1024)}, f32[4096]{0:T(1024)S(1)}, f32[768]{0:T(1024)}, f32[4096,768]{1,0:T(8,128)S(1)}) fusion(f32[4096,768]{1,0:T(8,128)} %copy-done.1, f32[4096]{0:T(1024)S(1)} %fusion.106, f32[4096]{0:T(1024)S(1)} %broadcast_multiply_fusion.1, f32[768]{0:T(1024)S(1)} %copy-done.63, bf16[4096,3072]{1,0:T(8,128)(2,1)} %get-tuple-element.153, ...), kind=kOutput, calls=%fused_computation.49 | convolution fusion | flops 19352514560 | bytes 55108608 | tf_op jit(solution)/shard_map/tf,df->td/dot_general | solution.py:174
  977.3 7.6 fusion.125
  985.0 16.7 fusion.124
  1003.5 15.7 copy.234
  1019.2 5.3 all-to-all-start.2
  1024.5 13.9 fusion.133
  1038.6 139.2 %all-to-all-done.2 = bf16[4,8,2,64,768]{4,2,1,0,3:T(2,128)(2,1)} async-done(((bf16[4,8,2,64,768]{4,2,1,0,3:T(2,128)(2,1)}), bf16[4,8,2,64,768]{4,2,1,0,3:T(2,128)(2,1)}, u32[]{:S(2)}, u32[]{:S(2)}) %all-to-all-start.2) | async-done | bytes 6291488 | tf_op jit(solution)/shard_map/all_to_all | solution.py:182
  1177.8 10.6 convert_reduce_fusion.1
  1188.4 6.3 copy.236
  1194.7 15.0 reshape.650
  1209.7 23.2 %fusion.72 = f32[2,2,8,96,96]{3,4,0,1,2:T(8,128)S(1)} fusion(bf16[256,2,8,8,96,1]{4,3,2,1,0,5:T(8,128)(2,1)} %bitcast.302, f32[256,1,8,8,96]{0,4,2,3,1:T(8,128)} %copy-done.2, f32[256,1,8,8,96]{0,4,2,3,1:T(8,128)} %fusion.155, f32[2,8,96]{2,1,0:T(8,128)S(1)} %copy-done.33), kind=kOutput, calls=%fused_computation.122 | convolution fusion | flops 1220542464 | bytes 20060160 | tf_op jit(solution)/shard_map/xakbi,xokbj->aobij/dot_general | solution.py:74
  1233.8 23.0 %convolution_bitcast_fusion.1 = f32[256,2,2,8,8,96]{0,5,3,4,2,1:T(8,128)} fusion(bf16[2,8,96,96,1,1]{3,2,5,1,0,4:T(8,128)(2,1)S(1)} %bitcast.319, bf16[256,2,8,8,96,1]{4,3,2,1,0,5:T(8,128)(2,1)} %bitcast.303), kind=kOutput, calls=%fused_computation.66 | convolution fusion | flops 1207959552 | bytes 31752192 | tf_op jit(solution)/shard_map/xokbj,cbij->xockbi/dot_general | solution.py:68
  1256.8 9.4 slice_add_fusion.1
  1267.8 6.6 fusion.58
  1277.2 12.8 fusion.67
  1293.1 29.1 %fusion.110 = f32[3072,768]{1,0:T(8,128)} fusion(bf16[4096,3072]{1,0:T(8,128)(2,1)} %get-tuple-element.123, f32[4096,768]{1,0:T(8,128)} %fusion.131), kind=kOutput, calls=%fused_computation.222 | convolution fusion | flops 19330498560 | bytes 47185920 | tf_op jit(solution)/shard_map/tf,td->fd/dot_general | solution.py:163
  1322.3 13.0 convolution_bitcast_fusion
  1335.2 11.3 fusion.32
  1351.3 6.4 add.421
  1360.2 6.4 copy.243
  1366.6 6.6 sub.163
  1377.7 15.7 copy.247
  1398.2 29.7 %fusion.115 = f32[768,3072]{1,0:T(8,128)} fusion(bf16[4096,3072]{1,0:T(8,128)(2,1)} %get-tuple-element.153, f32[4096,768]{1,0:T(8,128)} %copy-done.1, f32[768]{0:T(1024)S(1)} %copy-done.82, f32[768]{0:T(1024)S(1)} %copy-done.64, f32[4096]{0:T(1024)S(1)} %copy-done.55, f32[4096]{0:T(1024)S(1)} %copy-done.37), kind=kOutput, calls=%fused_computation.227 | convolution fusion | flops 19343081472 | bytes 47224832 | tf_op jit(solution)/shard_map/td,tf->df/dot_general | solution.py:172
  1428.0 114.7 %all-to-all-done.3 = bf16[4,64,2,8,768]{4,2,3,0,1:T(2,128)(2,1)} async-done(((bf16[4,64,2,8,768]{4,2,3,0,1:T(2,128)(2,1)}), bf16[4,64,2,8,768]{4,2,3,0,1:T(2,128)(2,1)}, u32[]{:S(2)}, u32[]{:S(2)}) %all-to-all-start.3) | async-done | bytes 6291488 | tf_op jit(solution)/shard_map/all_to_all | solution.py:196
  1542.7 9.9 fusion.39
  1552.7 20.1 %multiply_reduce_fusion.1 = (f32[768]{0:T(1024)S(1)}, f32[4096]{0:T(1024)S(1)}, f32[768]{0:T(1024)S(1)}, f32[4096,768]{1,0:T(8,128)}) fusion(f32[4096,768]{1,0:T(8,128)} %copy-done, f32[4096]{0:T(1024)S(1)} %copy-done.27, f32[4096]{0:T(1024)S(1)} %copy-done.21, f32[768]{0:T(1024)S(1)} %copy-done.43, f32[768]{0:T(1024)S(1)} %copy-done.53, ...), kind=kLoop, calls=%fused_computation.50 | loop fusion | flops 31451648 | bytes 50393088 | tf_op jit(solution)/shard_map/transpose(jvp())/reduce_sum | solution.py:17
  1572.9 12.6 fusion.123
  1585.5 6.2 convert_reduce_fusion.4
  1591.8 12.6 fusion.132
  1604.4 6.1 fusion.33
  1613.9 6.0 slice_add_fusion.3
  1630.5 5.5 convert_reduce_fusion.2
  1637.4 14.8 reduce-scatter.12.cloned.1.call-done
  1653.9 139.4 %reduce-scatter.10.cloned.1.call-done = f32[24,3072]{1,0:T(8,128)} async-done(((f32[768,3072]{1,0:T(8,128)}), f32[24,3072]{1,0:T(8,128)}) %reduce-scatter.10.cloned.1.call-update) | async-done | bytes 294928 | tf_op jit(solution)/shard_map/reduce_scatter | solution.py:221
  1795.2 40.1 %all-reduce.1 = f32[14,768]{1,0:T(8,128)S(1)} all-reduce(f32[14,768]{1,0:T(8,128)S(1)} %concatenate.15), channel_id=7, replica_groups=mesh['dp'=4,'wide'=8] {'dp','wide'}, use_global_device_ids=true, to_apply=%region_34.35.clone | all-reduce | flops 10752 | bytes 86016
  1836.0 66.3 %reduce-scatter.6.cloned.1.call-done = f32[40,768]{1,0:T(8,128)} async-done(((f32[1280,768]{1,0:T(8,128)}), f32[40,768]{1,0:T(8,128)}) %reduce-scatter.6.cloned.1.call-update) | async-done | bytes 122896 | tf_op jit(solution)/shard_map/reduce_scatter | solution.py:219
  1907.7 39.9 %all-reduce.2 = (f32[20]{0:T(128)S(1)}, f32[]{:T(128)}) all-reduce(f32[20]{0:T(128)S(1)} %copy-done.86, f32[]{:T(128)S(6)} %add.436), channel_id=1, replica_groups=mesh['dp'=4,'wide'=8] {'dp','wide'}, use_global_device_ids=true, to_apply=%region_6.7 | all-reduce | flops 21 | bytes 168 | tf_op jit(solution)/shard_map/psum | solution.py:319
  (319 shorter events, 96.5 us)
Async XLA Ops:
  7.2 86.6 %all-gather.6.cloned.1.call-start = ((), (), s32[]{:S(2)}) async-start(), calls=%async_computation.8 | async-start | bytes 2027520 | tf_op jit(solution)/shard_map/all_gather | solution.py:287
  80.6 604.2 %copy-start.17 = (bf16[128,2,64]{0,2,1:T(8,128)(2,1)}, bf16[128,2,64]{0,2,1:T(8,128)(2,1)S(1)}, u32[]{:S(2)}) copy-start(bf16[128,2,64]{0,2,1:T(8,128)(2,1)S(1)} %fusion.84) | copy-start | bytes 98308
  81.2 608.8 %copy-start.42 = (f32[768]{0:T(1024)}, f32[768]{0:T(1024)S(1)}, u32[]{:S(2)}) copy-start(f32[768]{0:T(1024)S(1)} %get-tuple-element.91) | copy-start | bytes 9220
  81.3 608.8 %copy-start.52 = (f32[768]{0:T(1024)}, f32[768]{0:T(1024)S(1)}, u32[]{:S(2)}) copy-start(f32[768]{0:T(1024)S(1)} %get-tuple-element.90) | copy-start | bytes 9220
  105.6 584.5 %copy-start.20 = (f32[4096]{0:T(1024)}, f32[4096]{0:T(1024)S(1)}, u32[]{:S(2)}) copy-start(f32[4096]{0:T(1024)S(1)} %broadcast_multiply_fusion.2) | copy-start | bytes 49156
  107.5 582.6 %copy-start.26 = (f32[4096]{0:T(1024)}, f32[4096]{0:T(1024)S(1)}, u32[]{:S(2)}) copy-start(f32[4096]{0:T(1024)S(1)} %fusion.105) | copy-start | bytes 49156
  118.6 221.3 %all-to-all-start = ((bf16[4,8,2,64,768]{4,1,0,2,3:T(8,128)(2,1)}), bf16[4,8,2,64,768]{4,1,0,2,3:T(8,128)(2,1)}, u32[]{:S(2)}, u32[]{:S(2)}) async-start(bf16[4,8,2,64,768]{4,1,0,2,3:T(8,128)(2,1)} %copy.216), calls=%async_computation | async-start | bytes 12582912 | tf_op jit(solution)/shard_map/all_to_all | solution.py:98
  123.3 580.9 %all-gather.8.cloned.1.call-start = ((), (), s32[]{:S(2)}) async-start(), calls=%async_computation.9 | async-start | bytes 4866048 | tf_op jit(solution)/shard_map/all_gather | solution.py:289
  124.3 215.4 %copy-start.57 = (f32[2,768]{1,0:T(2,128)}, f32[2,768]{1,0:T(2,128)S(1)}, u32[]{:S(2)}) copy-start(f32[2,768]{1,0:T(2,128)S(1)} %get-tuple-element.143) | copy-start | bytes 18436
  124.3 359.0 %copy-start.77 = (f32[2,768]{1,0:T(2,128)}, f32[2,768]{1,0:T(2,128)S(1)}, u32[]{:S(2)}) copy-start(f32[2,768]{1,0:T(2,128)S(1)} %get-tuple-element.142) | copy-start | bytes 18436
  339.7 68.7 %copy-start.32 = (f32[2,8,96]{2,1,0:T(8,128)}, f32[2,8,96]{2,1,0:T(8,128)S(1)}, u32[]{:S(2)}) copy-start(f32[2,8,96]{2,1,0:T(8,128)S(1)} %add.397) | copy-start | bytes 18436
  339.7 143.6 %copy-start.44 = (bf16[1,2,64,64]{3,2,1,0:T(8,128)(2,1)}, bf16[1,2,64,64]{3,2,1,0:T(8,128)(2,1)S(1)}, u32[]{:S(2)}) copy-start(bf16[1,2,64,64]{3,2,1,0:T(8,128)(2,1)S(1)} %get-tuple-element.146) | copy-start | bytes 49156
  339.8 143.6 %copy-start.46 = (bf16[1,2,64,64]{3,2,1,0:T(8,128)(2,1)}, bf16[1,2,64,64]{3,2,1,0:T(8,128)(2,1)S(1)}, u32[]{:S(2)}) copy-start(bf16[1,2,64,64]{3,2,1,0:T(8,128)(2,1)S(1)} %get-tuple-element.147) | copy-start | bytes 49156
  339.8 68.5 %copy-start.9 = (bf16[1,2,768,96]{3,2,1,0:T(8,128)(2,1)}, bf16[1,2,768,96]{3,2,1,0:T(8,128)(2,1)S(1)}, u32[]{:S(2)}) copy-start(bf16[1,2,768,96]{3,2,1,0:T(8,128)(2,1)S(1)} %get-tuple-element.140) | copy-start | bytes 884740
  501.7 183.1 %all-to-all-start.1 = ((bf16[4,64,2,8,768]{4,2,3,0,1:T(2,128)(2,1)}), bf16[4,64,2,8,768]{4,2,3,0,1:T(2,128)(2,1)}, u32[]{:S(2)}, u32[]{:S(2)}) async-start(bf16[4,64,2,8,768]{4,2,3,0,1:T(2,128)(2,1)} %copy.232), calls=%async_computation.1 | async-start | bytes 12582912 | tf_op jit(solution)/shard_map/all_to_all | solution.py:109
  506.6 333.1 %all-gather.10.cloned.1.call-start = ((), (), s32[]{:S(2)}) async-start(), calls=%async_computation.10 | async-start | bytes 4866048 | tf_op jit(solution)/shard_map/all_gather | solution.py:290
  507.4 360.0 %all-gather.12.cloned.1.call-start = ((), (), s32[]{:S(2)}) async-start(), calls=%async_computation.11 | async-start | bytes 2027520 | tf_op jit(solution)/shard_map/all_gather | solution.py:288
  698.3 279.0 %copy-start.36 = (f32[4096]{0:T(1024)}, f32[4096]{0:T(1024)S(1)}, u32[]{:S(2)}) copy-start(f32[4096]{0:T(1024)S(1)} %broadcast_multiply_fusion.1) | copy-start | bytes 49156
  704.2 135.5 %copy-start.40 = (f32[4096]{0:T(1024)}, f32[4096]{0:T(1024)S(1)}, u32[]{:S(2)}) copy-start(f32[4096]{0:T(1024)S(1)} %multiply_reduce_fusion.4) | copy-start | bytes 49156
  704.2 273.1 %copy-start.54 = (f32[4096]{0:T(1024)}, f32[4096]{0:T(1024)S(1)}, u32[]{:S(2)}) copy-start(f32[4096]{0:T(1024)S(1)} %fusion.106) | copy-start | bytes 49156
  704.3 135.4 %copy-start.83 = (f32[768]{0:T(1024)S(1)}, f32[768]{0:T(1024)}, u32[]{:S(2)}) copy-start(f32[768]{0:T(1024)} %get-tuple-element.86) | copy-start | bytes 9220
  1019.2 158.6 %all-to-all-start.2 = ((bf16[4,8,2,64,768]{4,2,1,0,3:T(2,128)(2,1)}), bf16[4,8,2,64,768]{4,2,1,0,3:T(2,128)(2,1)}, u32[]{:S(2)}, u32[]{:S(2)}) async-start(bf16[4,8,2,64,768]{4,2,1,0,3:T(2,128)(2,1)} %copy.234), calls=%async_computation.2 | async-start | bytes 12582912 | tf_op jit(solution)/shard_map/all_to_all | solution.py:182
  1024.5 153.3 %copy-start.45 = (bf16[1,2,64,64]{3,2,1,0:T(8,128)(2,1)S(1)}, bf16[1,2,64,64]{3,2,1,0:T(8,128)(2,1)}, u32[]{:S(2)}) copy-start(bf16[1,2,64,64]{3,2,1,0:T(8,128)(2,1)} %copy-done.44) | copy-start | bytes 49156
  1024.5 153.3 %copy-start.47 = (bf16[1,2,64,64]{3,2,1,0:T(8,128)(2,1)S(1)}, bf16[1,2,64,64]{3,2,1,0:T(8,128)(2,1)}, u32[]{:S(2)}) copy-start(bf16[1,2,64,64]{3,2,1,0:T(8,128)(2,1)} %copy-done.46) | copy-start | bytes 49156
  1024.5 153.3 %copy-start.78 = (f32[2,768]{1,0:T(2,128)S(1)}, f32[2,768]{1,0:T(2,128)}, u32[]{:S(2)}) copy-start(f32[2,768]{1,0:T(2,128)} %copy-done.77) | copy-start | bytes 18436
  1024.5 601.3 %reduce-scatter.8.cloned.1.call-start = ((), (), s32[]{:S(2)}) async-start(), calls=%async_computation.13 | async-start | bytes 4055040 | tf_op jit(solution)/shard_map/reduce_scatter | solution.py:220
  1038.5 597.4 %all-reduce.5.cloned.1.call-start = ((), (), s32[]{:S(2)}) async-start(), calls=%async_computation.16 | async-start | bytes 3145728
  1293.1 359.2 %reduce-scatter.12.cloned.1.call-start = ((), (), s32[]{:S(2)}) async-start(), calls=%async_computation.15 | async-start | bytes 9732096 | tf_op jit(solution)/shard_map/reduce_scatter | solution.py:222
  1393.4 149.3 %all-to-all-start.3 = ((bf16[4,64,2,8,768]{4,2,3,0,1:T(2,128)(2,1)}), bf16[4,64,2,8,768]{4,2,3,0,1:T(2,128)(2,1)}, u32[]{:S(2)}, u32[]{:S(2)}) async-start(bf16[4,64,2,8,768]{4,2,3,0,1:T(2,128)(2,1)} %copy.247), calls=%async_computation.3 | async-start | bytes 12582912 | tf_op jit(solution)/shard_map/all_to_all | solution.py:196
  1398.1 144.6 %copy-start.19 = (bf16[128,2,64]{0,2,1:T(8,128)(2,1)S(1)}, bf16[128,2,64]{0,2,1:T(8,128)(2,1)}, u32[]{:S(2)}) copy-start(bf16[128,2,64]{0,2,1:T(8,128)(2,1)} %copy-done.17) | copy-start | bytes 98308
  1398.1 395.2 %reduce-scatter.10.cloned.1.call-start = ((), (), s32[]{:S(2)}) async-start(), calls=%async_computation.14 | async-start | bytes 9732096 | tf_op jit(solution)/shard_map/reduce_scatter | solution.py:221
  1427.9 124.7 %copy-start.21 = (f32[4096]{0:T(1024)S(1)}, f32[4096]{0:T(1024)}, u32[]{:S(2)}) copy-start(f32[4096]{0:T(1024)} %copy-done.20) | copy-start | bytes 49156
  1427.9 124.7 %copy-start.27 = (f32[4096]{0:T(1024)S(1)}, f32[4096]{0:T(1024)}, u32[]{:S(2)}) copy-start(f32[4096]{0:T(1024)} %copy-done.26) | copy-start | bytes 49156
  1427.9 124.7 %copy-start.43 = (f32[768]{0:T(1024)S(1)}, f32[768]{0:T(1024)}, u32[]{:S(2)}) copy-start(f32[768]{0:T(1024)} %copy-done.42) | copy-start | bytes 9220
  1427.9 124.7 %copy-start.53 = (f32[768]{0:T(1024)S(1)}, f32[768]{0:T(1024)}, u32[]{:S(2)}) copy-start(f32[768]{0:T(1024)} %copy-done.52) | copy-start | bytes 9220
  1428.0 474.3 %reduce-scatter.6.cloned.1.call-start = ((), (), s32[]{:S(2)}) async-start(), calls=%async_computation.12 | async-start | bytes 4055040 | tf_op jit(solution)/shard_map/reduce_scatter | solution.py:219
  1542.7 30.1 %slice-start = ((s8[12582912]{0:T(1024)(128)(4,1)}), s8[4194304]{0:T(1024)(128)(4,1)S(1)}, s32[]{:S(2)}) async-start(s8[12582912]{0:T(1024)(128)(4,1)} %bitcast.298), calls=%async_computation.17 | async-start | bytes 8388608
  1552.7 32.8 %slice-start.3 = ((s8[12582912]{0:T(1024)(128)(4,1)}), s8[4194304]{0:T(1024)(128)(4,1)S(1)}, s32[]{:S(2)}) async-start(s8[12582912]{0:T(1024)(128)(4,1)} %bitcast.300), calls=%async_computation.20 | async-start | bytes 8388608
  1552.7 32.8 %slice-start.4 = ((s8[12582912]{0:T(1024)(128)(4,1)}), s8[4194304]{0:T(1024)(128)(4,1)S(1)}, s32[]{:S(2)}) async-start(s8[12582912]{0:T(1024)(128)(4,1)} %bitcast.300), calls=%async_computation.21 | async-start | bytes 8388608
  1629.9 319.8 %copy-start.61 = (f32[14,24]{1,0:T(8,128)S(1)}, f32[14,24]{1,0:T(8,128)}, u32[]{:S(2)}) copy-start(f32[14,24]{1,0:T(8,128)} %param.31) | copy-start | bytes 4036
  1629.9 321.2 %copy-start.23 = (f32[24,1280]{1,0:T(8,128)S(1)}, f32[24,1280]{1,0:T(8,128)}, u32[]{:S(2)}) copy-start(f32[24,1280]{1,0:T(8,128)} %param.27) | copy-start | bytes 368644
  1629.9 321.2 %copy-start.25 = (f32[24,1280]{1,0:T(8,128)S(1)}, f32[24,1280]{1,0:T(8,128)}, u32[]{:S(2)}) copy-start(f32[24,1280]{1,0:T(8,128)} %reduce-scatter.8.cloned.1.call-done) | copy-start | bytes 368644
  1629.9 322.0 %copy-start.24 = (f32[40,768]{1,0:T(8,128)S(1)}, f32[40,768]{1,0:T(8,128)}, u32[]{:S(2)}) copy-start(f32[40,768]{1,0:T(8,128)} %param.26) | copy-start | bytes 368644
  1630.2 164.8 %copy-start.67 = (f32[1,768]{1,0:T(1,128)S(1)}, f32[1,768]{1,0:T(1,128)}, u32[]{:S(2)}) copy-start(f32[1,768]{1,0:T(1,128)} %reshape.654) | copy-start | bytes 9220
  1630.2 164.8 %copy-start.68 = (f32[1,768]{1,0:T(1,128)S(1)}, f32[1,768]{1,0:T(1,128)}, u32[]{:S(2)}) copy-start(f32[1,768]{1,0:T(1,128)} %stack.90) | copy-start | bytes 9220
  1630.2 164.8 %copy-start.69 = (f32[1,768]{1,0:T(1,128)S(1)}, f32[1,768]{1,0:T(1,128)}, u32[]{:S(2)}) copy-start(f32[1,768]{1,0:T(1,128)} %reshape.655) | copy-start | bytes 9220
  1630.2 164.8 %copy-start.76 = (f32[2,768]{1,0:T(2,128)S(1)}, f32[2,768]{1,0:T(2,128)}, u32[]{:S(2)}) copy-start(f32[2,768]{1,0:T(2,128)} %get-tuple-element.154) | copy-start | bytes 18436
  1630.2 277.5 %copy-start.86 = (f32[20]{0:T(128)S(1)}, f32[20]{0:T(128)}, u32[]{:S(2)}) copy-start(f32[20]{0:T(128)} %reduce_sum.259) | copy-start | bytes 244
  1630.2 318.1 %copy-start.89 = (f32[20]{0:T(128)S(1)}, f32[20]{0:T(128)}, u32[]{:S(2)}) copy-start(f32[20]{0:T(128)} %copy-done.88) | copy-start | bytes 244
  1630.2 319.4 %copy-start.71 = (f32[14,24]{1,0:T(8,128)S(1)}, f32[14,24]{1,0:T(8,128)}, u32[]{:S(2)}) copy-start(f32[14,24]{1,0:T(8,128)} %param.37) | copy-start | bytes 4036
  1630.3 319.4 %copy-start.72 = (f32[14,24]{1,0:T(8,128)S(1)}, f32[14,24]{1,0:T(8,128)}, u32[]{:S(2)}) copy-start(f32[14,24]{1,0:T(8,128)} %param.43) | copy-start | bytes 4036
  1630.3 320.1 %copy-start.35 = (f32[2,2,24,96]{3,2,1,0:T(8,128)S(1)}, f32[2,2,24,96]{3,2,1,0:T(8,128)}, u32[]{:S(2)}) copy-start(f32[2,2,24,96]{3,2,1,0:T(8,128)} %param.30) | copy-start | bytes 110596
  1630.3 320.1 %copy-start.59 = (f32[2,2,24,96]{3,2,1,0:T(8,128)S(1)}, f32[2,2,24,96]{3,2,1,0:T(8,128)}, u32[]{:S(2)}) copy-start(f32[2,2,24,96]{3,2,1,0:T(8,128)} %param.36) | copy-start | bytes 110596
  1630.3 320.1 %copy-start.60 = (f32[2,2,24,96]{3,2,1,0:T(8,128)S(1)}, f32[2,2,24,96]{3,2,1,0:T(8,128)}, u32[]{:S(2)}) copy-start(f32[2,2,24,96]{3,2,1,0:T(8,128)} %param.42) | copy-start | bytes 110596
  1630.3 320.8 %copy-start.48 = (f32[24,1280]{1,0:T(8,128)S(1)}, f32[24,1280]{1,0:T(8,128)}, u32[]{:S(2)}) copy-start(f32[24,1280]{1,0:T(8,128)} %param.33) | copy-start | bytes 368644
  1630.3 320.7 %copy-start.49 = (f32[24,1280]{1,0:T(8,128)S(1)}, f32[24,1280]{1,0:T(8,128)}, u32[]{:S(2)}) copy-start(f32[24,1280]{1,0:T(8,128)} %param.39) | copy-start | bytes 368644
  1630.3 321.5 %copy-start.50 = (f32[40,768]{1,0:T(8,128)S(1)}, f32[40,768]{1,0:T(8,128)}, u32[]{:S(2)}) copy-start(f32[40,768]{1,0:T(8,128)} %param.32) | copy-start | bytes 368644
  1630.3 321.5 %copy-start.51 = (f32[40,768]{1,0:T(8,128)S(1)}, f32[40,768]{1,0:T(8,128)}, u32[]{:S(2)}) copy-start(f32[40,768]{1,0:T(8,128)} %param.38) | copy-start | bytes 368644
  1630.4 323.2 %copy-start.14 = (f32[96,768]{1,0:T(8,128)S(1)}, f32[96,768]{1,0:T(8,128)}, u32[]{:S(2)}) copy-start(f32[96,768]{1,0:T(8,128)} %param.29) | copy-start | bytes 884740
  1630.4 323.2 %copy-start.28 = (f32[96,768]{1,0:T(8,128)S(1)}, f32[96,768]{1,0:T(8,128)}, u32[]{:S(2)}) copy-start(f32[96,768]{1,0:T(8,128)} %param.35) | copy-start | bytes 884740
  1630.4 323.2 %copy-start.29 = (f32[96,768]{1,0:T(8,128)S(1)}, f32[96,768]{1,0:T(8,128)}, u32[]{:S(2)}) copy-start(f32[96,768]{1,0:T(8,128)} %param.41) | copy-start | bytes 884740
  1630.4 325.2 %copy-start.16 = (f32[24,3072]{1,0:T(8,128)S(1)}, f32[24,3072]{1,0:T(8,128)}, u32[]{:S(2)}) copy-start(f32[24,3072]{1,0:T(8,128)} %param.28) | copy-start | bytes 884740
  1630.4 325.2 %copy-start.30 = (f32[24,3072]{1,0:T(8,128)S(1)}, f32[24,3072]{1,0:T(8,128)}, u32[]{:S(2)}) copy-start(f32[24,3072]{1,0:T(8,128)} %param.34) | copy-start | bytes 884740
  1630.4 325.2 %copy-start.31 = (f32[24,3072]{1,0:T(8,128)S(1)}, f32[24,3072]{1,0:T(8,128)}, u32[]{:S(2)}) copy-start(f32[24,3072]{1,0:T(8,128)} %param.40) | copy-start | bytes 884740
  (48 other events, 670.4 us)
Sparse Core Ops, SparseCore 0:
  11.6 59.1 all-gather.5
  127.7 155.4 all-gather.7
  511.0 156.5 all-gather.9
  671.0 52.6 all-gather.11
  1038.6 158.2 reduce-scatter.7
  1293.2 159.4 all-reduce.4
  1458.6 193.5 reduce-scatter.11
  1658.2 135.1 reduce-scatter.9
  1798.8 103.4 reduce-scatter.5
where the time goes:
time: 1980 us; the launch traced here: 1970 us
  blocking collectives  540 us (27%)
  matrix products  519 us (26%)
  waiting for transfers between devices  475 us (24%)
  local copies, waits for them, and re-layouts  199 us (10%)
  other arithmetic  190 us (10%)
  between operations  23.3 us (1%)
  starting transfers between devices  20 us (1%)
    all_gather x1, blocking collectives, shards(): lax.all_gather(spectral_weight.astype(jnp.bfloat16), ('dp', 'wide'), axis...  215 us
    psum x1, blocking collectives, shards(): counts = lax.psum(local_counts, ('dp', 'wide'))  174 us
    reduce_scatter x1, waiting for transfers between devices, backward_layer(): lax.psum_scatter(grad_expand, ('dp', 'wide'), scatter_dimension=0, tiled=...  139 us
    all_to_all x1, waiting for transfers between devices, backward_layer(): lax.all_to_all(grad_cols, 'wide', split_axis=3, concat_axis=1, tiled=True)  139 us
    dot_general x1, matrix products, forward_layer(): jnp.dot(normed_two, expand_used, preferred_element_type=jnp.float32)  135 us
    all_to_all x1, waiting for transfers between devices, backward_layer(): lax.all_to_all(grad_rows, 'wide', split_axis=1, concat_axis=3, tiled=True)  115 us
    all_gather x1, blocking collectives, shards(): lax.all_gather(small_params.astype(jnp.bfloat16), ('dp', 'wide'), axis=1,...  70.5 us
    reduce_scatter x1, waiting for transfers between devices, backward_layer(): lax.psum_scatter(grad_embed, ('dp', 'wide'), scatter_dimension=0, tiled=T...  66.3 us
  transfers between devices with their start and end apart: 13, of which 5 were waited for; matrix products, arithmetic and copies ran while one was open for 36% of the time, Pallas kernels for 0%

commit v1 on v0

--- a/solution.py
+++ b/solution.py
@@ -9,6 +9,27 @@
 BETA_TWO = 0.95
 RATES = (0.08, 0.1, 0.1, 0.05, 0.3, 0.5)
 DECAYS = (0.1, 0.1, 0.1, 0.1, 0.1, 0.0)
+
+
+def in_order(parts, dim):
+    parts = jnp.moveaxis(parts, 0, dim)
+    lengths = parts.shape
+    return parts.reshape(*lengths[:dim], lengths[dim] * lengths[dim + 1], *lengths[dim + 2 :])
+
+
+def doubled(x, axis):
+    size, index = (lax.axis_size(axis), lax.axis_index(axis))
+    tiles, stride = (x[None], 1)
+    while stride < size:
+        other = lax.ppermute(tiles, axis, [(i, i ^ stride) for i in range(size)])
+        low = index & stride == 0
+        tiles = jnp.concatenate([jnp.where(low, tiles, other), jnp.where(low, other, tiles)])
+        stride *= 2
+    return tiles
+
+
+def collect(x, axis, dim):
+    return in_order(doubled(x, axis), dim)
 
 
 def layer_norm(values, gain, shift):
@@ -288,7 +309,7 @@
         lax.all_gather(head_weight.astype(jnp.bfloat16), ("dp", "wide"), axis=0, tiled=True),
         lax.all_gather(expand_weight.astype(jnp.bfloat16), ("dp", "wide"), axis=0, tiled=True),
         lax.all_gather(project_weight.astype(jnp.bfloat16), ("dp", "wide"), axis=0, tiled=True),
-        lax.all_gather(spectral_weight.astype(jnp.bfloat16), ("dp", "wide"), axis=2, tiled=True),
+        collect(spectral_weight.astype(jnp.bfloat16), ("dp", "wide"), 2),
         lax.all_gather(small_params.astype(jnp.bfloat16), ("dp", "wide"), axis=1, tiled=True),
     )
     used = tuple(gathered[:5]) + (gathered[5].astype(jnp.float32),)

time: 1980 us -> 1910 us (0.965)
  blocking collectives: 540 us -> 329 us
  waiting for transfers between devices: 475 us -> 620 us
    all_gather x1 -> x0, blocking collectives: 215 us -> none  [shards(): lax.all_gather(spectral_weight.astype(jnp.bfloat16), ('dp', 'wide'), axis...]
    ppermute x0 -> x5, waiting for transfers between devices: none -> 147 us  [doubled(): other = lax.ppermute(tiles, axis, [(i, i ^ stride) for i in range(size)])]
  transfers between devices with their start and end apart: 13 -> 18, of which waited for: 5 -> 10; matrix products, arithmetic and copies ran while one was open for 36% -> 37% of each run, Pallas kernels for 0% -> 0%
where the time goes in v1:
time: 1910 us; the launch traced here: 1900 us
  waiting for transfers between devices  620 us (32%)
  matrix products  502 us (26%)
  blocking collectives  329 us (17%)
  local copies, waits for them, and re-layouts  208 us (11%)
  other arithmetic  189 us (10%)
  starting transfers between devices  27.6 us (1%)
  between operations  23.3 us (1%)
    psum x1, blocking collectives, shards(): counts = lax.psum(local_counts, ('dp', 'wide'))  178 us
    ppermute x5, waiting for transfers between devices, doubled(): other = lax.ppermute(tiles, axis, [(i, i ^ stride) for i in range(size)])  147 us
    reduce_scatter x1, waiting for transfers between devices, backward_layer(): lax.psum_scatter(grad_expand, ('dp', 'wide'), scatter_dimension=0, tiled=...  139 us
    all_to_all x1, waiting for transfers between devices, backward_layer(): lax.all_to_all(grad_cols, 'wide', split_axis=3, concat_axis=1, tiled=True)  139 us
    dot_general x1, matrix products, forward_layer(): jnp.dot(normed_two, expand_used, preferred_element_type=jnp.float32)  135 us
    all_to_all x1, waiting for transfers between devices, backward_layer(): lax.all_to_all(grad_rows, 'wide', split_axis=1, concat_axis=3, tiled=True)  115 us
    all_gather x1, blocking collectives, shards(): lax.all_gather(small_params.astype(jnp.bfloat16), ('dp', 'wide'), axis=1,...  70.5 us
    reduce_scatter x1, waiting for transfers between devices, backward_layer(): lax.psum_scatter(grad_embed, ('dp', 'wide'), scatter_dimension=0, tiled=T...  66.2 us
  transfers between devices with their start and end apart: 18, of which 10 were waited for; matrix products, arithmetic and copies ran while one was open for 37% of the time, Pallas kernels for 0%

profile of v1, /device:TPU:0, one launch (start us, length us, event | category | flops | bytes accessed | tf_op | source)
XLA Modules:
  0.0 1898.9 jit_solution(8991765838692902379)
XLA Ops:
  9.5 70.5 %all-gather = bf16[32,24,14]{1,2,0:T(8,128)(2,1)S(1)} all-gather(bf16[1,24,14]{1,2,0:T(8,128)(2,1)S(1)} %convert_bitcast_fusion.4), channel_id=1, replica_groups=mesh['dp'=4,'wide'=8] {'dp','wide'}, dimensions={0}, use_global_device_ids=true | all-gather | bytes 22176 | tf_op jit(solution)/shard_map/all_gather | solution.py:313
  82.7 11.1 broadcast_multiply_fusion
  93.8 11.8 add_reduce_fusion
  112.7 6.2 copy.210
  125.6 46.6 %collective-permute-done = bf16[1,2,2,24,96]{4,3,0,2,1:T(8,128)(2,1)S(1)} collective-permute-done((bf16[1,2,2,24,96]{4,3,0,2,1:T(8,128)(2,1)S(1)}, bf16[1,2,2,24,96]{4,3,0,2,1:T(8,128)(2,1)S(1)}, u32[]{:S(2)}, u32[]{:S(2)}) %collective-permute-start) | collective-permute-done | bytes 18464 | tf_op jit(solution)/shard_map/ppermute | solution.py:24
  172.4 51.0 %collective-permute-done.1 = bf16[2,2,2,24,96]{4,3,0,2,1:T(8,128)(2,1)S(1)} collective-permute-done((bf16[2,2,2,24,96]{4,3,0,2,1:T(8,128)(2,1)S(1)}, bf16[2,2,2,24,96]{4,3,0,2,1:T(8,128)(2,1)S(1)}, u32[]{:S(2)}, u32[]{:S(2)}) %collective-permute-start.1) | collective-permute-done | bytes 36896 | tf_op jit(solution)/shard_map/ppermute | solution.py:24
  228.3 36.6 %collective-permute-done.2 = bf16[4,2,2,24,96]{4,3,0,2,1:T(8,128)(2,1)S(1)} collective-permute-done((bf16[4,2,2,24,96]{4,3,0,2,1:T(8,128)(2,1)S(1)}, bf16[4,2,2,24,96]{4,3,0,2,1:T(8,128)(2,1)S(1)}, u32[]{:S(2)}, u32[]{:S(2)}) %collective-permute-start.2) | collective-permute-done | bytes 73760 | tf_op jit(solution)/shard_map/ppermute | solution.py:24
  268.5 11.5 collective-permute-done.4
  280.4 7.1 fusion.22
  287.4 6.2 copy.212
  293.7 14.9 reshape.652
  308.5 11.9 copy.260
  320.5 12.9 convolution_bitcast_fusion.3
  333.4 6.2 fusion.154
  339.6 8.5 fusion.153
  348.1 10.6 convolution_bitcast_fusion.2
  358.8 14.9 slice_subtract_fusion.2
  373.7 8.3 copy.219
  382.0 9.6 sub.155
  391.6 7.4 copy.221
  399.0 8.3 copy.220
  407.3 9.7 add.405
  424.6 15.6 copy.224
  446.7 178.4 %psum.22 = f32[20]{0:T(128)S(1)} all-reduce(f32[20]{0:T(128)S(1)} %broadcast_multiply_fusion.3), channel_id=1, replica_groups=mesh['dp'=4,'wide'=8] {'dp','wide'}, use_global_device_ids=true, to_apply=%region_9.10 | all-reduce | flops 20 | bytes 160 | tf_op jit(solution)/shard_map/psum | solution.py:326
  632.2 8.1 fusion.123
  646.4 135.4 %multiply_convert_fusion = (bf16[4096,3072]{1,0:T(8,128)(2,1)}, f32[4096,3072]{1,0:T(8,128)}, f32[4096,3072]{1,0:T(8,128)}) fusion(f32[3072]{0:T(1024)S(1)} %add.414, bf16[768,3072]{1,0:T(8,128)(2,1)} %all-gather.8.cloned.1.call-done, f32[4096,768]{1,0:T(8,128)} %copy-done.1, f32[768]{0:T(1024)S(1)} %copy-done.85, f32[768]{0:T(1024)S(1)} %copy-done.67, ...), kind=kOutput, calls=%fused_computation.4 | convolution fusion | flops 20173553664 | bytes 143181824 | tf_op jit(solution)/shard_map/dot_general | solution.py:136
  781.9 27.6 %add_convert_fusion.2 = bf16[4096,768]{1,0:T(8,128)(2,1)} fusion(f32[4096,768]{1,0:T(8,128)} %copy-done.1, bf16[4096,3072]{1,0:T(8,128)(2,1)} %get-tuple-element.123, bf16[3072,768]{1,0:T(8,128)(2,1)} %all-gather.10.cloned.1.call-done, f32[768]{0:T(1024)S(1)} %copy-done.87), kind=kOutput, calls=%fused_computation.56 | convolution fusion | flops 19336790016 | bytes 48761856 | tf_op jit(solution)/shard_map/dot_general | solution.py:142
  809.6 16.8 fusion.10
  826.4 11.1 fusion.127
  837.4 54.3 %convert_reduce_fusion = (f32[3072]{0:T(1024)}, bf16[4096,3072]{1,0:T(8,128)(2,1)}) fusion(f32[4096,3072]{1,0:T(8,128)} %get-tuple-element.124, bf16[3072,768]{1,0:T(8,128)(2,1)} %all-gather.10.cloned.1.call-done, f32[4096,768]{1,0:T(8,128)} %fusion.127, f32[4096,3072]{1,0:T(8,128)} %get-tuple-element.160, f32[3072]{0:T(1024)S(1)} %add.414), kind=kOutput, calls=%fused_computation.2 | convolution fusion | flops 19544403968 | bytes 143155200 | tf_op jit(solution)/shard_map/td,fd->tf/dot_general | solution.py:188
  891.7 27.8 %multiply_reduce_fusion = (f32[768]{0:T(1024)}, f32[4096]{0:T(1024)S(1)}, f32[768]{0:T(1024)}, f32[4096,768]{1,0:T(8,128)S(1)}) fusion(f32[4096,768]{1,0:T(8,128)} %copy-done.1, f32[4096]{0:T(1024)S(1)} %fusion.102, f32[4096]{0:T(1024)S(1)} %broadcast_multiply_fusion.1, f32[768]{0:T(1024)S(1)} %copy-done.67, bf16[4096,3072]{1,0:T(8,128)(2,1)} %get-tuple-element.163, ...), kind=kOutput, calls=%fused_computation.49 | convolution fusion | flops 19352514560 | bytes 55108608 | tf_op jit(solution)/shard_map/tf,df->td/dot_general | solution.py:195
  919.5 7.4 fusion.121
  927.0 16.7 fusion.120
  945.6 15.6 copy.226
  966.6 13.9 fusion.129
  980.6 139.3 %all-to-all-done.2 = bf16[4,8,2,64,768]{4,2,1,0,3:T(2,128)(2,1)} async-done(((bf16[4,8,2,64,768]{4,2,1,0,3:T(2,128)(2,1)}), bf16[4,8,2,64,768]{4,2,1,0,3:T(2,128)(2,1)}, u32[]{:S(2)}, u32[]{:S(2)}) %all-to-all-start.2) | async-done | bytes 6291488 | tf_op jit(solution)/shard_map/all_to_all | solution.py:203
  1119.9 10.9 convert_reduce_fusion.1
  1130.8 6.3 copy.228
  1137.1 15.0 reshape.655
  1152.1 22.9 %fusion.68 = f32[2,2,8,96,96]{3,4,0,1,2:T(8,128)S(1)} fusion(bf16[256,2,8,8,96,1]{4,3,2,1,0,5:T(8,128)(2,1)} %bitcast.310, f32[256,1,8,8,96]{0,4,2,3,1:T(8,128)} %copy-done.2, f32[256,1,8,8,96]{0,4,2,3,1:T(8,128)} %copy-done.3, f32[2,8,96]{2,1,0:T(8,128)S(1)} %copy-done.36), kind=kOutput, calls=%fused_computation.120 | convolution fusion | flops 1220542464 | bytes 20060160 | tf_op jit(solution)/shard_map/xakbi,xokbj->aobij/dot_general | solution.py:95
  1175.9 23.1 %convolution_bitcast_fusion.1 = f32[256,2,2,8,8,96]{0,5,3,4,2,1:T(8,128)} fusion(bf16[2,8,96,96,1,1]{3,2,5,1,0,4:T(8,128)(2,1)S(1)} %bitcast.326, bf16[256,2,8,8,96,1]{4,3,2,1,0,5:T(8,128)(2,1)} %bitcast.311), kind=kOutput, calls=%fused_computation.66 | convolution fusion | flops 1207959552 | bytes 31752192 | tf_op jit(solution)/shard_map/xokbj,cbij->xockbi/dot_general | solution.py:89
  1199.0 9.4 slice_add_fusion.1
  1210.0 6.6 fusion.54
  1216.7 6.7 fusion.65
  1226.6 28.8 %fusion.106 = f32[3072,768]{1,0:T(8,128)} fusion(bf16[4096,3072]{1,0:T(8,128)(2,1)} %get-tuple-element.123, f32[4096,768]{1,0:T(8,128)} %fusion.127), kind=kOutput, calls=%fused_computation.236 | convolution fusion | flops 19330498560 | bytes 47185920 | tf_op jit(solution)/shard_map/tf,td->fd/dot_general | solution.py:184
  1255.5 13.1 convolution_bitcast_fusion
  1268.6 11.2 fusion.29
  1284.6 6.4 add.425
  1293.5 6.4 copy.235
  1300.0 6.6 sub.163
  1311.1 15.7 copy.239
  1331.6 29.8 %fusion.111 = f32[768,3072]{1,0:T(8,128)} fusion(bf16[4096,3072]{1,0:T(8,128)(2,1)} %get-tuple-element.163, f32[4096,768]{1,0:T(8,128)} %copy-done.1, f32[768]{0:T(1024)S(1)} %copy-done.86, f32[768]{0:T(1024)S(1)} %copy-done.68, f32[4096]{0:T(1024)S(1)} %copy-done.59, f32[4096]{0:T(1024)S(1)} %copy-done.39), kind=kOutput, calls=%fused_computation.241 | convolution fusion | flops 19343081472 | bytes 47224832 | tf_op jit(solution)/shard_map/td,tf->df/dot_general | solution.py:193
  1361.5 114.6 %all-to-all-done.3 = bf16[4,64,2,8,768]{4,2,3,0,1:T(2,128)(2,1)} async-done(((bf16[4,64,2,8,768]{4,2,3,0,1:T(2,128)(2,1)}), bf16[4,64,2,8,768]{4,2,3,0,1:T(2,128)(2,1)}, u32[]{:S(2)}, u32[]{:S(2)}) %all-to-all-start.3) | async-done | bytes 6291488 | tf_op jit(solution)/shard_map/all_to_all | solution.py:217
  1476.1 9.9 fusion.36
  1486.1 20.9 %multiply_reduce_fusion.1 = (f32[768]{0:T(1024)S(1)}, f32[4096]{0:T(1024)S(1)}, f32[768]{0:T(1024)S(1)}, f32[4096,768]{1,0:T(8,128)}) fusion(f32[4096,768]{1,0:T(8,128)} %copy-done, f32[4096]{0:T(1024)S(1)} %copy-done.30, f32[4096]{0:T(1024)S(1)} %copy-done.22, f32[768]{0:T(1024)S(1)} %copy-done.45, f32[768]{0:T(1024)S(1)} %copy-done.57, ...), kind=kLoop, calls=%fused_computation.50 | loop fusion | flops 31451648 | bytes 50393088 | tf_op jit(solution)/shard_map/transpose(jvp())/reduce_sum | solution.py:38
  1507.0 12.3 fusion.119
  1519.4 6.2 convert_reduce_fusion.4
  1525.6 12.7 fusion.128
  1547.6 6.0 slice_add_fusion.3
  1571.1 13.6 reduce-scatter.12.cloned.1.call-done
  1586.4 139.4 %reduce-scatter.10.cloned.1.call-done = f32[24,3072]{1,0:T(8,128)} async-done(((f32[768,3072]{1,0:T(8,128)}), f32[24,3072]{1,0:T(8,128)}) %reduce-scatter.10.cloned.1.call-update) | async-done | bytes 294928 | tf_op jit(solution)/shard_map/reduce_scatter | solution.py:242
  1727.7 40.1 %all-reduce.1 = f32[14,768]{1,0:T(8,128)S(1)} all-reduce(f32[14,768]{1,0:T(8,128)S(1)} %concatenate.35), channel_id=7, replica_groups=mesh['dp'=4,'wide'=8] {'dp','wide'}, use_global_device_ids=true, to_apply=%region_34.35.clone | all-reduce | flops 10752 | bytes 86016
  1768.5 66.2 %reduce-scatter.6.cloned.1.call-done = f32[40,768]{1,0:T(8,128)} async-done(((f32[1280,768]{1,0:T(8,128)}), f32[40,768]{1,0:T(8,128)}) %reduce-scatter.6.cloned.1.call-update) | async-done | bytes 122896 | tf_op jit(solution)/shard_map/reduce_scatter | solution.py:240
  1840.1 39.8 %all-reduce.2 = (f32[20]{0:T(128)S(1)}, f32[]{:T(128)}) all-reduce(f32[20]{0:T(128)S(1)} %copy-done.90, f32[]{:T(128)S(6)} %add.440), channel_id=1, replica_groups=mesh['dp'=4,'wide'=8] {'dp','wide'}, use_global_device_ids=true, to_apply=%region_6.7 | all-reduce | flops 21 | bytes 168 | tf_op jit(solution)/shard_map/psum | solution.py:340
  (347 shorter events, 125.0 us)
Async XLA Ops:
  7.2 86.6 %all-gather.6.cloned.1.call-start = ((), (), s32[]{:S(2)}) async-start(), calls=%async_computation.8 | async-start | bytes 2027520 | tf_op jit(solution)/shard_map/all_gather | solution.py:308
  80.4 184.6 %copy-start.37 = (f32[768,14]{0,1:T(8,128)}, f32[768,14]{0,1:T(8,128)S(1)}, u32[]{:S(2)}) copy-start(f32[768,14]{0,1:T(8,128)S(1)} %reshape.665) | copy-start | bytes 129028
  80.6 546.8 %copy-start.18 = (bf16[128,2,64]{0,2,1:T(8,128)(2,1)}, bf16[128,2,64]{0,2,1:T(8,128)(2,1)S(1)}, u32[]{:S(2)}) copy-start(bf16[128,2,64]{0,2,1:T(8,128)(2,1)S(1)} %fusion.80) | copy-start | bytes 98308
  81.3 550.9 %copy-start.44 = (f32[768]{0:T(1024)}, f32[768]{0:T(1024)S(1)}, u32[]{:S(2)}) copy-start(f32[768]{0:T(1024)S(1)} %get-tuple-element.91) | copy-start | bytes 9220
  81.3 550.9 %copy-start.56 = (f32[768]{0:T(1024)}, f32[768]{0:T(1024)S(1)}, u32[]{:S(2)}) copy-start(f32[768]{0:T(1024)S(1)} %get-tuple-element.90) | copy-start | bytes 9220
  105.6 526.6 %copy-start.21 = (f32[4096]{0:T(1024)}, f32[4096]{0:T(1024)S(1)}, u32[]{:S(2)}) copy-start(f32[4096]{0:T(1024)S(1)} %broadcast_multiply_fusion.2) | copy-start | bytes 49156
  107.5 524.7 %copy-start.29 = (f32[4096]{0:T(1024)}, f32[4096]{0:T(1024)S(1)}, u32[]{:S(2)}) copy-start(f32[4096]{0:T(1024)S(1)} %fusion.101) | copy-start | bytes 49156
  112.7 114.8 %copy-start.16 = (f32[24,3072]{1,0:T(8,128)S(1)}, f32[24,3072]{1,0:T(8,128)}, u32[]{:S(2)}) copy-start(f32[24,3072]{1,0:T(8,128)} %param.28) | copy-start | bytes 884740
  118.9 161.5 %all-to-all-start = ((bf16[4,8,2,64,768]{4,1,0,2,3:T(8,128)(2,1)}), bf16[4,8,2,64,768]{4,1,0,2,3:T(8,128)(2,1)}, u32[]{:S(2)}, u32[]{:S(2)}) async-start(bf16[4,8,2,64,768]{4,1,0,2,3:T(8,128)(2,1)} %copy.210), calls=%async_computation | async-start | bytes 12582912 | tf_op jit(solution)/shard_map/all_to_all | solution.py:119
  123.6 522.8 %all-gather.8.cloned.1.call-start = ((), (), s32[]{:S(2)}) async-start(), calls=%async_computation.9 | async-start | bytes 4866048 | tf_op jit(solution)/shard_map/all_gather | solution.py:310
  123.7 48.5 %collective-permute-start = (bf16[1,2,2,24,96]{4,3,0,2,1:T(8,128)(2,1)S(1)}, bf16[1,2,2,24,96]{4,3,0,2,1:T(8,128)(2,1)S(1)}, u32[]{:S(2)}, u32[]{:S(2)}) collective-permute-start(bf16[1,2,2,24,96]{4,3,0,2,1:T(8,128)(2,1)S(1)} %convert_bitcast_fusion.2), channel_id=1, source_target_pairs={{0,1},{1,0},{2,3},{3,2},{4,5},{5,4},{6,7},{7,6},{8,9},{9,8},{10,11... | collective-permute-start | bytes 55304 | tf_op jit(solution)/shard_map/ppermute | solution.py:24
  172.2 51.2 %collective-permute-start.1 = (bf16[2,2,2,24,96]{4,3,0,2,1:T(8,128)(2,1)S(1)}, bf16[2,2,2,24,96]{4,3,0,2,1:T(8,128)(2,1)S(1)}, u32[]{:S(2)}, u32[]{:S(2)}) collective-permute-start(bf16[2,2,2,24,96]{4,3,0,2,1:T(8,128)(2,1)S(1)} %pad_maximum_fusion.3), channel_id=1, source_target_pairs={{0,2},{1,3},{2,0},{3,1},{4,6},{5,7},{6,4},{7,5},{8,10},{9,11},{10,... | collective-permute-start | bytes 110600 | tf_op jit(solution)/shard_map/ppermute | solution.py:24
  223.5 41.4 %collective-permute-start.2 = (bf16[4,2,2,24,96]{4,3,0,2,1:T(8,128)(2,1)S(1)}, bf16[4,2,2,24,96]{4,3,0,2,1:T(8,128)(2,1)S(1)}, u32[]{:S(2)}, u32[]{:S(2)}) collective-permute-start(bf16[4,2,2,24,96]{4,3,0,2,1:T(8,128)(2,1)S(1)} %pad_maximum_fusion.2), channel_id=1, source_target_pairs={{0,4},{1,5},{2,6},{3,7},{4,0},{5,1},{6,2},{7,3},{8,12},{9,13},{10,... | collective-permute-start | bytes 221192 | tf_op jit(solution)/shard_map/ppermute | solution.py:24
  265.0 1.5 collective-permute-start.3
  265.1 156.7 %copy-start.81 = (f32[2,768]{1,0:T(2,128)}, f32[2,768]{1,0:T(2,128)S(1)}, u32[]{:S(2)}) copy-start(f32[2,768]{1,0:T(2,128)S(1)} %get-tuple-element.150) | copy-start | bytes 18436
  265.2 82.9 %copy-start.35 = (f32[2,8,96]{2,1,0:T(8,128)}, f32[2,8,96]{2,1,0:T(8,128)S(1)}, u32[]{:S(2)}) copy-start(f32[2,8,96]{2,1,0:T(8,128)S(1)} %add.401) | copy-start | bytes 18436
  266.6 13.3 collective-permute-start.4
  440.2 187.2 %all-to-all-start.1 = ((bf16[4,64,2,8,768]{4,2,3,0,1:T(2,128)(2,1)}), bf16[4,64,2,8,768]{4,2,3,0,1:T(2,128)(2,1)}, u32[]{:S(2)}, u32[]{:S(2)}) async-start(bf16[4,64,2,8,768]{4,2,3,0,1:T(2,128)(2,1)} %copy.224), calls=%async_computation.1 | async-start | bytes 12582912 | tf_op jit(solution)/shard_map/all_to_all | solution.py:130
  445.0 336.9 %all-gather.10.cloned.1.call-start = ((), (), s32[]{:S(2)}) async-start(), calls=%async_computation.10 | async-start | bytes 4866048 | tf_op jit(solution)/shard_map/all_gather | solution.py:311
  445.7 363.8 %all-gather.12.cloned.1.call-start = ((), (), s32[]{:S(2)}) async-start(), calls=%async_computation.11 | async-start | bytes 2027520 | tf_op jit(solution)/shard_map/all_gather | solution.py:309
  640.4 279.1 %copy-start.38 = (f32[4096]{0:T(1024)}, f32[4096]{0:T(1024)S(1)}, u32[]{:S(2)}) copy-start(f32[4096]{0:T(1024)S(1)} %broadcast_multiply_fusion.1) | copy-start | bytes 49156
  646.3 135.5 %copy-start.42 = (f32[4096]{0:T(1024)}, f32[4096]{0:T(1024)S(1)}, u32[]{:S(2)}) copy-start(f32[4096]{0:T(1024)S(1)} %multiply_reduce_fusion.4) | copy-start | bytes 49156
  646.4 273.2 %copy-start.58 = (f32[4096]{0:T(1024)}, f32[4096]{0:T(1024)S(1)}, u32[]{:S(2)}) copy-start(f32[4096]{0:T(1024)S(1)} %fusion.102) | copy-start | bytes 49156
  646.4 135.4 %copy-start.87 = (f32[768]{0:T(1024)S(1)}, f32[768]{0:T(1024)}, u32[]{:S(2)}) copy-start(f32[768]{0:T(1024)} %get-tuple-element.86) | copy-start | bytes 9220
  961.2 158.7 %all-to-all-start.2 = ((bf16[4,8,2,64,768]{4,2,1,0,3:T(2,128)(2,1)}), bf16[4,8,2,64,768]{4,2,1,0,3:T(2,128)(2,1)}, u32[]{:S(2)}, u32[]{:S(2)}) async-start(bf16[4,8,2,64,768]{4,2,1,0,3:T(2,128)(2,1)} %copy.226), calls=%async_computation.2 | async-start | bytes 12582912 | tf_op jit(solution)/shard_map/all_to_all | solution.py:203
  966.5 153.4 %copy-start.48 = (bf16[1,2,64,64]{3,2,1,0:T(8,128)(2,1)S(1)}, bf16[1,2,64,64]{3,2,1,0:T(8,128)(2,1)}, u32[]{:S(2)}) copy-start(bf16[1,2,64,64]{3,2,1,0:T(8,128)(2,1)} %copy-done.46) | copy-start | bytes 49156
  966.5 153.4 %copy-start.51 = (bf16[1,2,64,64]{3,2,1,0:T(8,128)(2,1)S(1)}, bf16[1,2,64,64]{3,2,1,0:T(8,128)(2,1)}, u32[]{:S(2)}) copy-start(bf16[1,2,64,64]{3,2,1,0:T(8,128)(2,1)} %copy-done.49) | copy-start | bytes 49156
  966.6 153.3 %copy-start.82 = (f32[2,768]{1,0:T(2,128)S(1)}, f32[2,768]{1,0:T(2,128)}, u32[]{:S(2)}) copy-start(f32[2,768]{1,0:T(2,128)} %copy-done.81) | copy-start | bytes 18436
  966.6 593.0 %reduce-scatter.8.cloned.1.call-start = ((), (), s32[]{:S(2)}) async-start(), calls=%async_computation.13 | async-start | bytes 4055040 | tf_op jit(solution)/shard_map/reduce_scatter | solution.py:241
  980.6 589.0 %all-reduce.5.cloned.1.call-start = ((), (), s32[]{:S(2)}) async-start(), calls=%async_computation.16 | async-start | bytes 3145728
  1226.6 358.2 %reduce-scatter.12.cloned.1.call-start = ((), (), s32[]{:S(2)}) async-start(), calls=%async_computation.15 | async-start | bytes 9732096 | tf_op jit(solution)/shard_map/reduce_scatter | solution.py:243
  1326.8 149.3 %all-to-all-start.3 = ((bf16[4,64,2,8,768]{4,2,3,0,1:T(2,128)(2,1)}), bf16[4,64,2,8,768]{4,2,3,0,1:T(2,128)(2,1)}, u32[]{:S(2)}, u32[]{:S(2)}) async-start(bf16[4,64,2,8,768]{4,2,3,0,1:T(2,128)(2,1)} %copy.239), calls=%async_computation.3 | async-start | bytes 12582912 | tf_op jit(solution)/shard_map/all_to_all | solution.py:217
  1331.5 144.6 %copy-start.20 = (bf16[128,2,64]{0,2,1:T(8,128)(2,1)S(1)}, bf16[128,2,64]{0,2,1:T(8,128)(2,1)}, u32[]{:S(2)}) copy-start(bf16[128,2,64]{0,2,1:T(8,128)(2,1)} %copy-done.18) | copy-start | bytes 98308
  1331.5 394.3 %reduce-scatter.10.cloned.1.call-start = ((), (), s32[]{:S(2)}) async-start(), calls=%async_computation.14 | async-start | bytes 9732096 | tf_op jit(solution)/shard_map/reduce_scatter | solution.py:242
  1361.4 124.6 %copy-start.22 = (f32[4096]{0:T(1024)S(1)}, f32[4096]{0:T(1024)}, u32[]{:S(2)}) copy-start(f32[4096]{0:T(1024)} %copy-done.21) | copy-start | bytes 49156
  1361.4 124.6 %copy-start.30 = (f32[4096]{0:T(1024)S(1)}, f32[4096]{0:T(1024)}, u32[]{:S(2)}) copy-start(f32[4096]{0:T(1024)} %copy-done.29) | copy-start | bytes 49156
  1361.4 124.6 %copy-start.45 = (f32[768]{0:T(1024)S(1)}, f32[768]{0:T(1024)}, u32[]{:S(2)}) copy-start(f32[768]{0:T(1024)} %copy-done.44) | copy-start | bytes 9220
  1361.4 124.6 %copy-start.57 = (f32[768]{0:T(1024)S(1)}, f32[768]{0:T(1024)}, u32[]{:S(2)}) copy-start(f32[768]{0:T(1024)} %copy-done.56) | copy-start | bytes 9220
  1361.4 473.3 %reduce-scatter.6.cloned.1.call-start = ((), (), s32[]{:S(2)}) async-start(), calls=%async_computation.12 | async-start | bytes 4055040 | tf_op jit(solution)/shard_map/reduce_scatter | solution.py:240
  1563.7 318.3 %copy-start.65 = (f32[14,24]{1,0:T(8,128)S(1)}, f32[14,24]{1,0:T(8,128)}, u32[]{:S(2)}) copy-start(f32[14,24]{1,0:T(8,128)} %param.31) | copy-start | bytes 4036
  1563.7 319.7 %copy-start.24 = (f32[24,1280]{1,0:T(8,128)S(1)}, f32[24,1280]{1,0:T(8,128)}, u32[]{:S(2)}) copy-start(f32[24,1280]{1,0:T(8,128)} %param.27) | copy-start | bytes 368644
  1563.7 319.7 %copy-start.26 = (f32[24,1280]{1,0:T(8,128)S(1)}, f32[24,1280]{1,0:T(8,128)}, u32[]{:S(2)}) copy-start(f32[24,1280]{1,0:T(8,128)} %reduce-scatter.8.cloned.1.call-done) | copy-start | bytes 368644
  1563.7 320.5 %copy-start.25 = (f32[40,768]{1,0:T(8,128)S(1)}, f32[40,768]{1,0:T(8,128)}, u32[]{:S(2)}) copy-start(f32[40,768]{1,0:T(8,128)} %param.26) | copy-start | bytes 368644
  1564.0 163.5 %copy-start.71 = (f32[1,768]{1,0:T(1,128)S(1)}, f32[1,768]{1,0:T(1,128)}, u32[]{:S(2)}) copy-start(f32[1,768]{1,0:T(1,128)} %reshape.659) | copy-start | bytes 9220
  1564.0 163.5 %copy-start.72 = (f32[1,768]{1,0:T(1,128)S(1)}, f32[1,768]{1,0:T(1,128)}, u32[]{:S(2)}) copy-start(f32[1,768]{1,0:T(1,128)} %stack.90) | copy-start | bytes 9220
  1564.0 163.5 %copy-start.73 = (f32[1,768]{1,0:T(1,128)S(1)}, f32[1,768]{1,0:T(1,128)}, u32[]{:S(2)}) copy-start(f32[1,768]{1,0:T(1,128)} %reshape.660) | copy-start | bytes 9220
  1564.0 163.5 %copy-start.80 = (f32[2,768]{1,0:T(2,128)S(1)}, f32[2,768]{1,0:T(2,128)}, u32[]{:S(2)}) copy-start(f32[2,768]{1,0:T(2,128)} %get-tuple-element.164) | copy-start | bytes 18436
  1564.0 276.1 %copy-start.90 = (f32[20]{0:T(128)S(1)}, f32[20]{0:T(128)}, u32[]{:S(2)}) copy-start(f32[20]{0:T(128)} %reduce_sum.259) | copy-start | bytes 244
  1564.0 316.6 %copy-start.93 = (f32[20]{0:T(128)S(1)}, f32[20]{0:T(128)}, u32[]{:S(2)}) copy-start(f32[20]{0:T(128)} %copy-done.92) | copy-start | bytes 244
  1564.1 317.9 %copy-start.75 = (f32[14,24]{1,0:T(8,128)S(1)}, f32[14,24]{1,0:T(8,128)}, u32[]{:S(2)}) copy-start(f32[14,24]{1,0:T(8,128)} %param.37) | copy-start | bytes 4036
  1564.1 317.9 %copy-start.76 = (f32[14,24]{1,0:T(8,128)S(1)}, f32[14,24]{1,0:T(8,128)}, u32[]{:S(2)}) copy-start(f32[14,24]{1,0:T(8,128)} %param.43) | copy-start | bytes 4036
  1564.1 318.6 %copy-start.28 = (f32[2,2,24,96]{3,2,1,0:T(8,128)S(1)}, f32[2,2,24,96]{3,2,1,0:T(8,128)}, u32[]{:S(2)}) copy-start(f32[2,2,24,96]{3,2,1,0:T(8,128)} %param.30) | copy-start | bytes 110596
  1564.1 318.6 %copy-start.63 = (f32[2,2,24,96]{3,2,1,0:T(8,128)S(1)}, f32[2,2,24,96]{3,2,1,0:T(8,128)}, u32[]{:S(2)}) copy-start(f32[2,2,24,96]{3,2,1,0:T(8,128)} %param.36) | copy-start | bytes 110596
  1564.1 318.6 %copy-start.64 = (f32[2,2,24,96]{3,2,1,0:T(8,128)S(1)}, f32[2,2,24,96]{3,2,1,0:T(8,128)}, u32[]{:S(2)}) copy-start(f32[2,2,24,96]{3,2,1,0:T(8,128)} %param.42) | copy-start | bytes 110596
  1564.1 319.3 %copy-start.52 = (f32[24,1280]{1,0:T(8,128)S(1)}, f32[24,1280]{1,0:T(8,128)}, u32[]{:S(2)}) copy-start(f32[24,1280]{1,0:T(8,128)} %param.33) | copy-start | bytes 368644
  1564.1 319.3 %copy-start.53 = (f32[24,1280]{1,0:T(8,128)S(1)}, f32[24,1280]{1,0:T(8,128)}, u32[]{:S(2)}) copy-start(f32[24,1280]{1,0:T(8,128)} %param.39) | copy-start | bytes 368644
  1564.1 320.0 %copy-start.54 = (f32[40,768]{1,0:T(8,128)S(1)}, f32[40,768]{1,0:T(8,128)}, u32[]{:S(2)}) copy-start(f32[40,768]{1,0:T(8,128)} %param.32) | copy-start | bytes 368644
  1564.1 320.0 %copy-start.55 = (f32[40,768]{1,0:T(8,128)S(1)}, f32[40,768]{1,0:T(8,128)}, u32[]{:S(2)}) copy-start(f32[40,768]{1,0:T(8,128)} %param.38) | copy-start | bytes 368644
  1564.2 321.7 %copy-start.15 = (f32[96,768]{1,0:T(8,128)S(1)}, f32[96,768]{1,0:T(8,128)}, u32[]{:S(2)}) copy-start(f32[96,768]{1,0:T(8,128)} %param.29) | copy-start | bytes 884740
  1564.2 321.7 %copy-start.31 = (f32[96,768]{1,0:T(8,128)S(1)}, f32[96,768]{1,0:T(8,128)}, u32[]{:S(2)}) copy-start(f32[96,768]{1,0:T(8,128)} %param.35) | copy-start | bytes 884740
  1564.2 321.7 %copy-start.32 = (f32[96,768]{1,0:T(8,128)S(1)}, f32[96,768]{1,0:T(8,128)}, u32[]{:S(2)}) copy-start(f32[96,768]{1,0:T(8,128)} %param.41) | copy-start | bytes 884740
  1564.2 323.7 %copy-start.17 = (f32[24,3072]{1,0:T(8,128)S(1)}, f32[24,3072]{1,0:T(8,128)}, u32[]{:S(2)}) copy-start(f32[24,3072]{1,0:T(8,128)} %param.28) | copy-start | bytes 884740
  1564.2 323.7 %copy-start.33 = (f32[24,3072]{1,0:T(8,128)S(1)}, f32[24,3072]{1,0:T(8,128)}, u32[]{:S(2)}) copy-start(f32[24,3072]{1,0:T(8,128)} %param.34) | copy-start | bytes 884740
  1564.2 323.7 %copy-start.34 = (f32[24,3072]{1,0:T(8,128)S(1)}, f32[24,3072]{1,0:T(8,128)}, u32[]{:S(2)}) copy-start(f32[24,3072]{1,0:T(8,128)} %param.40) | copy-start | bytes 884740
  (57 other events, 972.8 us)
Sparse Core Ops, SparseCore 0:
  11.6 59.1 all-gather.5
  228.4 80.2 all-gather.7
  449.3 159.4 all-gather.9
  612.2 53.7 all-gather.11
  980.7 157.6 reduce-scatter.7
  1226.7 158.9 all-reduce.4
  1391.6 193.1 reduce-scatter.11
  1590.7 135.1 reduce-scatter.9
  1731.2 103.4 reduce-scatter.5
